TPU v7x, 32 devices: a whole 2x2x4 slice. The times are simulated.
32 devices in a mesh: mp: 4 (over z), dp: 8 (over y, x, core).
Axes of the slice: x: 2, y: 2, z: 4, core: 2. Of those that a mesh axis runs over, the one named last changes fastest.
Arguments:
- a_mat: bfloat16 [3072, 196608], P(('mp', 'dp'))
- b_mat: bfloat16 [196608, 768], P(('mp', 'dp'))
Outputs:
- output: bfloat16 [3072, 768], P(('mp', 'dp'))
All inputs are finite; a program needn't handle non-finite values.
Results may differ from a plain program's by a relative error of at most 0.001.
Values are sent between devices in bfloat16 or wider.
A program may use at most 1 GiB of HBM per device.

v0:
```python
import jax
import jax.numpy as jnp
from jax import lax
from jax.sharding import PartitionSpec as P


def solution(mesh):
    mp_size = mesh.shape["mp"]
    dp_size = mesh.shape["dp"]

    def local_product(a_rows, b_rows):
        row_count = a_rows.shape[0]
        tok_piece = b_rows.shape[0]
        a_split = a_rows.reshape(row_count, mp_size, dp_size, tok_piece)
        a_cols = lax.all_to_all(a_split, "dp", 2, 0, tiled=True)
        a_cols = a_cols.reshape(row_count * dp_size, mp_size, tok_piece)
        b_group = lax.all_gather(b_rows, "mp", axis=0, tiled=False)
        part_sum = jnp.einsum("rit,itn->rn", a_cols, b_group, preferred_element_type=jnp.float32)
        row_sum = lax.psum_scatter(part_sum, "dp", scatter_dimension=0, tiled=True)
        return row_sum.astype(jnp.bfloat16)

    return jax.shard_map(
        local_product,
        mesh=mesh,
        in_specs=(P(("mp", "dp"), None), P(("mp", "dp"), None)),
        out_specs=P(("mp", "dp"), None),
        check_vma=False,
    )
```

profile of v0, /device:TPU:0, one launch (start us, length us, event | category | flops | bytes accessed | tf_op | source)
XLA Modules:
  0.0 731.2 jit_solution(7086246714356942670)
XLA Ops:
  6.5 0.0 all-gather.3.cloned.1.call-start
  6.5 0.7 all-gather.3.cloned.1.call-update
  7.3 0.0 reduce-scatter.2.cloned.1.call-start
  7.3 33.4 %copy.7 = bf16[12,8,32,6144]{3,2,1,0:T(8,128)(2,1)} copy(bf16[12,8,32,6144]{3,1,2,0:T(8,128)(2,1)} %bitcast.14) | data formatting | bytes 75497472
  40.7 33.7 %copy.5 = bf16[96,4,8,6144]{3,0,1,2:T(8,128)(2,1)} copy(bf16[96,4,8,6144]{3,2,1,0:T(8,128)(2,1)} %bitcast.13) | data formatting | bytes 75497472 | tf_op jit(solution)/shard_map/reshape | solution.py:14
  74.5 421.1 %all_to_all.15 = bf16[96,4,8,6144]{3,0,1,2:T(8,128)(2,1)} all-to-all(bf16[96,4,8,6144]{3,0,1,2:T(8,128)(2,1)} %copy.5), channel_id=1, replica_groups=mesh['mp'=4,'dp'=8] {'dp'}, dimensions={2} | all-to-all | bytes 75497472 | tf_op jit(solution)/shard_map/all_to_all | solution.py:15
  495.5 25.4 %copy.6 = bf16[8,96,4,1,6144]{4,1,0,2,3:T(8,128)(2,1)} copy(bf16[8,96,4,1,6144]{4,1,2,0,3:T(8,128)(2,1)} %bitcast.12) | data formatting | bytes 75497472 | tf_op jit(solution)/shard_map/all_to_all | solution.py:15
  520.9 123.1 %all-gather.3.cloned.1.call-done = bf16[24576,768]{1,0:T(8,128)(2,1)} async-done(((bf16[6144,768]{1,0:T(8,128)(2,1)}), bf16[24576,768]{1,0:T(8,128)(2,1)}) %all-gather.3.cloned.1.call-update) | async-done | bytes 37748752 | tf_op jit(solution)/shard_map/all_gather | solution.py:17
  644.0 37.7 %convolution_bitcast_fusion = f32[768,768]{1,0:T(8,128)} fusion(bf16[768,4,6144]{2,0,1:T(8,128)(2,1)} %bitcast.15, bf16[4,6144,768]{2,1,0:T(8,128)(2,1)} %bitcast.16), kind=kOutput, calls=%fused_computation | convolution fusion | flops 28991029248 | bytes 77856768 | tf_op jit(solution)/shard_map/rit,itn->rn/dot_general | solution.py:18
  681.7 0.0 reduce-scatter.2.cloned.1.call-update
  681.7 41.0 %reduce-scatter.2.cloned.1.call-done = f32[96,768]{1,0:T(8,128)} async-done(((f32[768,768]{1,0:T(8,128)}), f32[96,768]{1,0:T(8,128)}) %reduce-scatter.2.cloned.1.call-update) | async-done | bytes 294928 | tf_op jit(solution)/shard_map/reduce_scatter | solution.py:19
  722.7 1.6 convert_element_type.3
Async XLA Ops:
  6.5 637.4 %all-gather.3.cloned.1.call-start = ((), (), s32[]{:S(2)}) async-start(), calls=%async_computation.3 | async-start | bytes 47185920 | tf_op jit(solution)/shard_map/all_gather | solution.py:17
  7.3 715.5 %reduce-scatter.2.cloned.1.call-start = ((), (), s32[]{:S(2)}) async-start(), calls=%async_computation.2 | async-start | bytes 2654208 | tf_op jit(solution)/shard_map/reduce_scatter | solution.py:19
Sparse Core Ops, SparseCore 0:
  8.9 635.0 all-gather.2
  681.8 40.8 reduce-scatter.1
where the time goes:
time: 732 us; the launch traced here: 731 us
  blocking collectives  421 us (58%)
  waiting for transfers between devices  165 us (23%)
  local copies, waits for them, and re-layouts  92.6 us (13%)
  matrix products  37.7 us (5%)
  between operations  13.4 us (2%)
    all_to_all x1, blocking collectives, local_product(): a_cols = lax.all_to_all(a_split, 'dp', 2, 0, tiled=True)  421 us
    all_gather x1, waiting for transfers between devices, local_product(): b_group = lax.all_gather(b_rows, 'mp', axis=0, tiled=False)  123 us
    reduce_scatter x1, waiting for transfers between devices, local_product(): row_sum = lax.psum_scatter(part_sum, 'dp', scatter_dimension=0, tiled=True)  41 us
    dot_general x1, matrix products, local_product(): jnp.einsum('rit,itn->rn', a_cols, b_group, preferred_element_type=jnp.flo...  37.7 us
    reshape x1, local copies, waits for them, and re-layouts, local_product(): a_split = a_rows.reshape(row_count, mp_size, dp_size, tok_piece)  33.7 us
    unnamed x1, local copies, waits for them, and re-layouts  33.4 us
    all_to_all x1, local copies, waits for them, and re-layouts, local_product(): a_cols = lax.all_to_all(a_split, 'dp', 2, 0, tiled=True)  25.4 us
  transfers between devices with their start and end apart: 2, of which 2 were waited for; matrix products, arithmetic and copies ran while one was open for 13% of the time, Pallas kernels for 0%

commit v1 on v0

v1 whole, which is shorter than its diff:
```python
import functools

import jax
import jax.numpy as jnp
from jax import lax
from jax.experimental import pallas as pl
from jax.experimental.pallas import tpu as pltpu
from jax.sharding import PartitionSpec as P

MESH = pl.DeviceIdType.MESH
CHUNKS = 24
AHEAD = 3
STOCK = 3


def mask_bits(pos):
    return (pos >> 1) & 1, pos & 1, pos >> 2


def flip(bit, by):
    return 1 - bit if by else bit


def kernel(
    n, a_ref, b_ref, c_ref, ra, rx, r0, r1, fa,
    acc, acc2, va, vb, core_in, plane_in, core_in2, plane_in2, back,
    send_a, recv_a, send_o, recv_o, send_x, recv_x, load_sem, rs_send, rs_recv, back_sem,
):
    z, dp = lax.axis_index("mp"), lax.axis_index("dp")
    y, x, core = dp // 4, (dp // 2) % 2, dp % 2
    rows = a_ref.shape[0]
    tok = b_ref.shape[0]
    kc = tok // n
    slots = 2 * n
    high = z // 2
    is_mid = ((z + 1) // 2) % 2 == 1
    is_end = jnp.logical_not(is_mid)
    pair = (z // 2) * 2 + (1 - z % 2)
    across = 3 - z
    peers = []
    for pos in range(1, 8):
        my, mx, mc = mask_bits(pos)
        peers.append(flip(y, my) * 4 + flip(x, mx) * 2 + flip(core, mc))

    def block_of(near):
        return near + high * (3 - 2 * near)

    def a_cols(u, w, owner):
        phase = u // n
        near = 2 + phase if w else 1 - phase
        start = (block_of(near) * 8 + owner) * tok + (u % n) * kc
        return pl.ds(pl.multiple_of(start, kc), kc)

    def at(i):
        return pl.ds(pl.multiple_of(i * kc, kc), kc)

    def a_send(u, w, pos):
        return pltpu.make_async_remote_copy(
            src_ref=a_ref.at[:, a_cols(u, w, peers[pos - 1])],
            dst_ref=ra.at[w, pl.ds((pos - 1) * rows, rows), at(u)],
            send_sem=send_a.at[u],
            recv_sem=recv_a.at[u],
            device_id=(z, peers[pos - 1]),
            device_id_type=MESH,
        )

    def exchange_a(u):
        for w in range(2):
            for pos in (3, 7, 1, 2, 5, 6, 4):
                a_send(u, w, pos).start()

    def wait(ref, sem):
        pltpu.make_async_copy(ref, ref, sem).wait()

    def wait_sent_a(u):
        wait(ra.at[:, :, at(u)], send_a.at[u])

    def to_pair(src, dst, slot):
        return pltpu.make_async_remote_copy(
            src_ref=src, dst_ref=dst, send_sem=send_o.at[slot], recv_sem=recv_o.at[slot],
            device_id=(pair, dp), device_id_type=MESH,
        )

    def to_across(src, u):
        return pltpu.make_async_remote_copy(
            src_ref=src, dst_ref=rx.at[at(u)], send_sem=send_x.at[u], recv_sem=recv_x.at[u],
            device_id=(across, dp), device_id_type=MESH,
        )

    @pl.when(is_mid)
    def _():
        to_across(b_ref.at[at(0)], 0).start()
        to_pair(b_ref.at[at(0)], r1, 0).start()
        to_across(b_ref.at[at(1)], 1).start()

    @pl.when(is_end)
    def _():
        for j in range(STOCK):
            to_pair(b_ref.at[at(j)], r0.at[at(j)], j).start()

    for u in range(AHEAD):
        exchange_a(u)

    acc[...] = jnp.zeros_like(acc)
    acc2[...] = jnp.zeros_like(acc2)

    def load_a(u, w, slot):
        own = pltpu.make_async_copy(
            a_ref.at[:, a_cols(u, w, dp)], va.at[slot, pl.ds(0, rows)], load_sem.at[slot, 0]
        )
        others = pltpu.make_async_copy(
            ra.at[w, :, at(u)], va.at[slot, pl.ds(rows, 7 * rows)], load_sem.at[slot, 1]
        )
        own.start()
        others.start()

    def load_fa(i, slot):
        pltpu.make_async_copy(fa.at[:, at(i)], va.at[slot], load_sem.at[slot, 0]).start()

    def load_b(src, slot):
        pltpu.make_async_copy(src, vb.at[slot], load_sem.at[slot, 2]).start()

    def product(total, slot):
        size = (8 * rows) // 4

        def part(r, carry):
            at_r = pl.ds(pl.multiple_of(r * size, size), size)
            total[at_r] += jnp.dot(va[slot, at_r], vb[slot], preferred_element_type=jnp.float32)
            return carry

        lax.fori_loop(0, 4, part, 0)

    def core_step(total, landing, k):
        my = flip(core, 1)
        return pltpu.make_async_remote_copy(
            src_ref=total.at[pl.ds(4 * rows, 4 * rows)], dst_ref=landing,
            send_sem=rs_send.at[k, 0], recv_sem=rs_recv.at[k, 0],
            device_id=(z, y * 4 + x * 2 + my), device_id_type=MESH,
        )

    def plane_step(total, landing, k, pos):
        return pltpu.make_async_remote_copy(
            src_ref=total.at[pl.ds(pos * rows, rows)], dst_ref=landing.at[pos - 1],
            send_sem=rs_send.at[k, pos], recv_sem=rs_recv.at[k, pos],
            device_id=(z, peers[pos - 1]), device_id_type=MESH,
        )

    def step(t, carry):
        @pl.when(is_mid)
        def _():
            @pl.when(t < slots)
            def _():
                wait(rx.at[at(t)], recv_x.at[t])
                to_pair(rx.at[at(t)], rx.at[at(t)], t + 1).start()

            @pl.when(t < slots - 1)
            def _():
                wait(r0.at[at(0)], recv_o.at[t])

            @pl.when(jnp.logical_and(t >= n - 1, t < slots - 1))
            def _():
                to_across(r0.at[at(t - n + 1)], t + 1).start()

            @pl.when(t + 2 < n)
            def _():
                to_across(b_ref.at[at(t + 2)], t + 2).start()

        @pl.when(is_end)
        def _():
            wait(r1, recv_o.at[t])

            @pl.when(jnp.logical_and(t >= STOCK + n - 2, t < slots - 2))
            def _():
                j = t - n + 2
                to_pair(b_ref.at[at(j)], r0.at[at(j)], t + 1).start()

        u = t - 1

        @pl.when(t >= 1)
        def _():
            wait(ra.at[:, :, at(u)], recv_a.at[u])

        @pl.when(jnp.logical_and(is_end, jnp.logical_and(t + 1 >= STOCK, t + 1 < STOCK + n - 1)))
        def _():
            i = t + 2 - STOCK
            to_pair(a_ref.at[:, a_cols(i, 0, dp)], fa.at[pl.ds(0, rows), at(i)], t + 1).start()
            to_pair(ra.at[0, :, at(i)], fa.at[pl.ds(rows, 7 * rows), at(i)], t + 1).start()

        @pl.when(t + AHEAD < slots)
        def _():
            wait_sent_a(t)
            exchange_a(t + AHEAD)

        first = jnp.logical_and(t >= 1, jnp.logical_or(is_mid, jnp.logical_or(t == 1, u >= n)))
        third = jnp.logical_and(is_mid, jnp.logical_and(t >= STOCK, t < STOCK + n - 1))

        @pl.when(t >= 1)
        def _():
            load_a(u, 1, 1)
            load_b(rx.at[at(u)], 1)

        @pl.when(first)
        def _():
            load_a(u, 0, 0)

            @pl.when(is_mid)
            def _():
                @pl.when(u < n)
                def _():
                    load_b(b_ref.at[at(u)], 0)

                @pl.when(u >= n)
                def _():
                    load_b(r0.at[at(u - n)], 0)

            @pl.when(is_end)
            def _():
                @pl.when(u < n)
                def _():
                    load_b(r1, 0)

                @pl.when(u >= n)
                def _():
                    load_b(b_ref.at[at(u - n)], 0)

        @pl.when(third)
        def _():
            i = t - STOCK + 1
            load_fa(i, 2)
            load_b(b_ref.at[at(i)], 2)

        def wait_load(slot, parts):
            if parts == 3:
                wait(va.at[slot, pl.ds(0, rows)], load_sem.at[slot, 0])
                wait(va.at[slot, pl.ds(rows, 7 * rows)], load_sem.at[slot, 1])
            else:
                wait(va.at[slot], load_sem.at[slot, 0])
            wait(vb.at[slot], load_sem.at[slot, 2])

        @pl.when(first)
        def _():
            wait_load(0, 3)
            product(acc, 0)

        @pl.when(third)
        def _():
            wait_load(2, 2)
            product(acc2, 2)

        @pl.when(t >= 1)
        def _():
            wait_load(1, 3)
            product(acc, 1)

        done = STOCK + n - 2

        @pl.when(jnp.logical_and(is_mid, t == done + 1))
        def _():
            core_step(acc2, core_in2, 0).start()

        @pl.when(jnp.logical_and(is_mid, t == done + 2))
        def _():
            core_step(acc2, core_in2, 0).wait()
            acc2[pl.ds(0, 4 * rows)] += core_in2[...]

        @pl.when(jnp.logical_and(is_mid, t == done + 3))
        def _():
            for pos in (3, 1, 2):
                plane_step(acc2, plane_in2, 0, pos).start()

        @pl.when(jnp.logical_and(is_mid, t == done + 6))
        def _():
            for pos in (3, 1, 2):
                plane_step(acc2, plane_in2, 0, pos).wait()
            acc2[pl.ds(0, rows)] += (plane_in2[0] + plane_in2[1]) + plane_in2[2]

        return carry

    lax.fori_loop(0, slots + 1, step, 0)

    core_copy = core_step(acc, core_in, 1)
    core_copy.start()
    back_copy = pltpu.make_async_remote_copy(
        src_ref=acc2.at[pl.ds(0, rows)], dst_ref=back, send_sem=back_sem.at[0], recv_sem=back_sem.at[1],
        device_id=(pair, dp), device_id_type=MESH,
    )

    @pl.when(is_mid)
    def _():
        back_copy.start()

    core_copy.wait()
    acc[pl.ds(rows, 3 * rows)] += core_in[pl.ds(rows, 3 * rows)]
    plane_copies = [plane_step(acc, plane_in, 1, pos) for pos in (3, 1, 2)]
    for copy in plane_copies:
        copy.start()
    total = acc[pl.ds(0, rows)] + core_in[pl.ds(0, rows)]

    def sent_a(u, carry):
        wait_sent_a(u)
        return carry

    lax.fori_loop(slots - AHEAD, slots, sent_a, 0)

    @pl.when(is_mid)
    def _():
        def sent(s, carry):
            wait(rx.at[at(0)], send_x.at[s])
            return carry

        lax.fori_loop(0, slots, sent, 0)

        def sent_o(s, carry):
            wait(rx.at[at(0)], send_o.at[s])
            return carry

        lax.fori_loop(0, slots + 1, sent_o, 0)

    @pl.when(is_end)
    def _():
        def sent_o(s, carry):
            wait(rx.at[at(0)], send_o.at[s])
            return carry

        lax.fori_loop(0, slots - 1, sent_o, 0)

    for copy in plane_copies:
        copy.wait()
    total += (plane_in[0] + plane_in[1]) + plane_in[2]

    @pl.when(is_mid)
    def _():
        back_copy.wait_send()
        c_ref[...] = total.astype(c_ref.dtype)

    @pl.when(is_end)
    def _():
        back_copy.wait_recv()
        c_ref[...] = (total + back[...]).astype(c_ref.dtype)


def solution(mesh):
    n = CHUNKS

    def local_product(a_rows, b_rows):
        rows, tok, cols = a_rows.shape[0], b_rows.shape[0], b_rows.shape[1]
        kc = tok // n
        slots = 2 * n
        bf16, f32 = jnp.bfloat16, jnp.float32
        hbm = pl.BlockSpec(memory_space=pltpu.HBM)
        out = pl.pallas_call(
            functools.partial(kernel, n),
            name="product",
            out_shape=(
                jax.ShapeDtypeStruct((rows, cols), bf16),
                jax.ShapeDtypeStruct((2, 7 * rows, 2 * tok), bf16),
                jax.ShapeDtypeStruct((2 * tok, cols), bf16),
                jax.ShapeDtypeStruct((tok, cols), bf16),
                jax.ShapeDtypeStruct((kc, cols), bf16),
                jax.ShapeDtypeStruct((8 * rows, tok), bf16),
            ),
            in_specs=[hbm, hbm],
            out_specs=(pl.BlockSpec(memory_space=pltpu.VMEM), hbm, hbm, hbm, hbm, hbm),
            scratch_shapes=[
                pltpu.VMEM((8 * rows, cols), f32),
                pltpu.VMEM((8 * rows, cols), f32),
                pltpu.VMEM((3, 8 * rows, kc), bf16),
                pltpu.VMEM((3, kc, cols), bf16),
                pltpu.VMEM((4 * rows, cols), f32),
                pltpu.VMEM((3, rows, cols), f32),
                pltpu.VMEM((4 * rows, cols), f32),
                pltpu.VMEM((3, rows, cols), f32),
                pltpu.VMEM((rows, cols), f32),
                pltpu.SemaphoreType.DMA((slots,)),
                pltpu.SemaphoreType.DMA((slots,)),
                pltpu.SemaphoreType.DMA((slots + 1,)),
                pltpu.SemaphoreType.DMA((slots + 1,)),
                pltpu.SemaphoreType.DMA((slots,)),
                pltpu.SemaphoreType.DMA((slots,)),
                pltpu.SemaphoreType.DMA((3, 3)),
                pltpu.SemaphoreType.DMA((2, 4)),
                pltpu.SemaphoreType.DMA((2, 4)),
                pltpu.SemaphoreType.DMA((2,)),
            ],
            compiler_params=pltpu.CompilerParams(has_side_effects=True),
        )(a_rows, b_rows)
        return out[0]

    return jax.shard_map(
        local_product,
        mesh=mesh,
        in_specs=(P(("mp", "dp"), None), P(("mp", "dp"), None)),
        out_specs=P(("mp", "dp"), None),
        check_vma=False,
    )
```

time: 732 us -> 460 us (0.63)
  Pallas kernels: 0 us -> 457 us
  blocking collectives: 421 us -> 0 us
  waiting for transfers between devices: 165 us -> 0 us
  local copies, waits for them, and re-layouts: 92.6 us -> 1.58 us
  matrix products: 37.7 us -> 0 us
  between operations: 13.4 us -> 0.01 us
    pallas_call x0 -> x1, Pallas kernels: none -> 457 us  [local_product(): pl.pallas_call(functools.partial(kernel, n), name='product', out_shape=(j...]
    all_to_all x1 -> x0, blocking collectives: 421 us -> none  [local_product(): a_cols = lax.all_to_all(a_split, 'dp', 2, 0, tiled=True)]
    all_gather x1 -> x0, waiting for transfers between devices: 123 us -> none  [local_product(): b_group = lax.all_gather(b_rows, 'mp', axis=0, tiled=False)]
    reduce_scatter x1 -> x0, waiting for transfers between devices: 41 us -> none  [local_product(): row_sum = lax.psum_scatter(part_sum, 'dp', scatter_dimension=0, tiled=True)]
    dot_general x1 -> x0, matrix products: 37.7 us -> none  [local_product(): jnp.einsum('rit,itn->rn', a_cols, b_group, preferred_element_type=jnp.flo...]
    reshape x1 -> x0, local copies, waits for them, and re-layouts: 33.7 us -> none  [local_product(): a_split = a_rows.reshape(row_count, mp_size, dp_size, tok_piece)]
    unnamed x1, local copies, waits for them, and re-layouts: 33.4 us -> 1.58 us
    all_to_all x1 -> x0, local copies, waits for them, and re-layouts: 25.4 us -> none  [local_product(): a_cols = lax.all_to_all(a_split, 'dp', 2, 0, tiled=True)]
  transfers between devices with their start and end apart: 2 -> 0, of which waited for: 2 -> 0; matrix products, arithmetic and copies ran while one was open for 13% -> 0% of each run, Pallas kernels for 0% -> 0%
where the time goes in v1:
time: 460 us; the launch traced here: 458 us
  Pallas kernels  457 us (99%)
    pallas_call x1, Pallas kernels, local_product(): pl.pallas_call(functools.partial(kernel, n), name='product', out_shape=(j...  457 us

profile of v1, /device:TPU:0, one launch (start us, length us, event | category | flops | bytes accessed | tf_op | source)
XLA Modules:
  0.0 458.1 jit_solution(17333002368351593228)
XLA Ops:
  0.0 456.5 %product.1 = (bf16[96,768]{1,0:T(8,128)(2,1)}, bf16[2,672,12288]{2,1,0:T(8,128)(2,1)}, bf16[12288,768]{1,0:T(8,128)(2,1)}, bf16[6144,768]{1,0:T(8,128)(2,1)}, bf...) custom-call(bf16[96,196608]{1,0:T(8,128)(2,1)} %a_ref.1, bf16[6144,768]{1,0:T(8,128)(2,1)} %b_ref.1), custom_call_target="tpu_custom_call" | custom-call | tf_op jit(solution)/shard_map/product/pallas_call | solution.py:351
  456.5 1.6 copy.4
